TPU v7x, 32 devices: a whole 2x2x4 slice. The times are simulated.
32 devices in a mesh: expert: 4 (over y, x), shard: 8 (over z, core).
Axes of the slice: x: 2, y: 2, z: 4, core: 2. Of those that a mesh axis runs over, the one named last changes fastest.
Arguments:
- tokens: bfloat16 [256, 6144], P(('expert', 'shard')), may hold values from -6 to 6
- norm_gain: float32 [6144], replicated, may hold values from 0.5 to 1.5
- routes: int32 [256, 2], P(('expert', 'shard')), may hold values from 0 to 3, all different within a row; in each aligned block of 8 rows (0 to 7, 8 to 15, ...) at most 4 rows name the same one
- gate_weights: float32 [256, 2], P(('expert', 'shard')), may hold values from 0.2 to 1
- capacity: int32 [4], replicated, may hold values from 2 to 4
- w_gate: bfloat16 [4, 6144, 8192], P('expert', None, 'shard'), may hold values from -0.078125 to 0.078125
- w_up: bfloat16 [4, 6144, 8192], P('expert', None, 'shard'), may hold values from -0.078125 to 0.078125
- w_down: bfloat16 [4, 8192, 6144], P('expert', 'shard'), may hold values from -0.0625 to 0.0625
Outputs:
- mixed_out: bfloat16 [256, 6144], P(('expert', 'shard'))
Inputs may be any that keep to these rules, and one draw needn't show every extreme that they name: `routes`: each row names 2 different experts; among the rows of one device no expert is named by more than 4 rows.
All inputs are finite; a program needn't handle non-finite values.
Results may differ from a plain program's by a relative error of at most 0.019.
Values may be sent and summed in bfloat16 or wider, within the bound.
A program may use at most 128 MiB of HBM per device.

v0:
```python
import jax
import jax.numpy as jnp
from jax import lax
from jax.sharding import PartitionSpec as P


def rms_norm(tokens, norm_gain):
    widened = tokens.astype(jnp.float32)
    mean_square = jnp.mean(widened * widened, axis=-1, keepdims=True)
    return (widened * lax.rsqrt(mean_square + 1e-05) * norm_gain).astype(jnp.bfloat16)


def slot_ranks(blocked):
    equal_ids = blocked[:, :, None, :, None] == blocked[:, None, :, None, :]
    shared = jnp.any(equal_ids, axis=4).astype(jnp.int32)
    per_block = blocked.shape[1]
    positions = jnp.arange(per_block, dtype=jnp.int32)
    earlier = (positions[None, :] < positions[:, None]).astype(jnp.int32)
    return jnp.sum(shared * earlier[None, :, :, None], axis=2)


def on_device(tokens, norm_gain, routes, gate_weights, capacity, w_gate, w_up, w_down):
    normed = rms_norm(tokens, norm_gain)
    tok_count = tokens.shape[0]
    expert_count = capacity.shape[0]
    slot_depth = max(tok_count // 2, tok_count * routes.shape[1] // expert_count)
    slot_rank = slot_ranks(routes[None])[0]
    expert_ids = jnp.arange(expert_count, dtype=jnp.int32)
    is_expert = routes[:, :, None] == expert_ids
    limit_rows = jnp.sum(jnp.where(is_expert, capacity, 0), axis=-1)
    kept_mask = slot_rank < limit_rows
    slot_ids = jnp.arange(slot_depth, dtype=jnp.int32)
    matched = (
        is_expert[:, :, :, None]
        & (slot_rank[:, :, None, None] == slot_ids)
        & kept_mask[:, :, None, None]
    )
    picker = jnp.sum(matched.astype(jnp.float32), axis=1).astype(jnp.bfloat16)
    buffers = jnp.einsum("tej,td->ejd", picker, normed, preferred_element_type=jnp.float32).astype(
        jnp.bfloat16
    )
    combine = jnp.sum(jnp.where(matched, gate_weights[:, :, None, None], jnp.float32(0.0)), axis=1)
    gate_proj = w_gate[0]
    up_proj = w_up[0]
    down_proj = w_down[0]
    arrived = lax.all_to_all(buffers, "expert", split_axis=0, concat_axis=0, tiled=True)
    slot_rows = lax.all_gather(arrived[None], "shard", axis=0, tiled=True)
    row_shape = slot_rows.shape
    flat_rows = slot_rows.reshape(-1, row_shape[-1])
    gate_val = jnp.dot(flat_rows, gate_proj, preferred_element_type=jnp.float32)
    up_val = jnp.dot(flat_rows, up_proj, preferred_element_type=jnp.float32)
    hidden = (jax.nn.silu(gate_val) * up_val).astype(jnp.bfloat16)
    partial_out = jnp.dot(hidden, down_proj, preferred_element_type=jnp.float32)
    partial_value = partial_out.reshape(row_shape[:-1] + (down_proj.shape[1],))
    rounded_parts = partial_value.astype(jnp.bfloat16)
    pieces = lax.all_to_all(
        lax.all_to_all(rounded_parts, "expert", split_axis=1, concat_axis=1, tiled=True),
        "shard",
        split_axis=0,
        concat_axis=0,
        tiled=True,
    )
    returned = jnp.sum(pieces.astype(jnp.float32), axis=0).astype(jnp.bfloat16)
    mixed_out = jnp.einsum(
        "tej,ejd->td", combine, returned.astype(jnp.float32), precision=lax.Precision.HIGHEST
    )
    return mixed_out.astype(jnp.bfloat16)


def solution(mesh):
    in_specs = (
        P(("expert", "shard"), None),
        P(),
        P(("expert", "shard"), None),
        P(("expert", "shard"), None),
        P(),
        P("expert", None, "shard"),
        P("expert", None, "shard"),
        P("expert", "shard", None),
    )
    out_specs = P(("expert", "shard"), None)
    return jax.shard_map(
        on_device, mesh=mesh, in_specs=in_specs, out_specs=out_specs, check_vma=False
    )
```

profile of v0, /device:TPU:0, one launch (start us, length us, event | category | flops | bytes accessed | tf_op | source)
XLA Modules:
  0.0 144.9 jit_solution(16787414954088235093)
XLA Ops:
  6.5 0.0 all-gather.3.cloned.1.call-start
  6.5 1.1 fusion.17
  7.6 0.8 compare_reduce_fusion
  8.4 0.8 select_reduce_fusion.2
  9.2 0.1 select_reduce_fusion.1
  9.4 0.7 iota_compare_fusion
  10.1 0.7 convert_reduce_fusion
  10.8 1.1 convolution_convert_fusion
  11.9 10.6 %all_to_all.15 = bf16[4,4,6144]{2,1,0:T(4,128)(2,1)} all-to-all(bf16[4,4,6144]{2,1,0:T(4,128)(2,1)S(1)} %convolution_convert_fusion), channel_id=1, replica_groups=mesh['expert'=4,'shard'=8] {'expert'}, dimensions={0} | all-to-all | bytes 393216 | tf_op jit(solution)/shard_map/all_to_all | solution.py:46
  22.6 0.0 all-gather.3.cloned.1.call-update
  22.6 25.0 %all-gather.3.cloned.1.call-done = bf16[32,4,6144]{2,1,0:T(4,128)(2,1)} async-done(((bf16[4,4,6144]{2,1,0:T(4,128)(2,1)}), bf16[32,4,6144]{2,1,0:T(4,128)(2,1)}) %all-gather.3.cloned.1.call-update) | async-done | bytes 1572880 | tf_op jit(solution)/shard_map/all_gather | solution.py:47
  47.6 2.7 %reshape.66 = bf16[128,6144]{1,0:T(8,128)(2,1)S(1)} reshape(bf16[32,4,6144]{2,1,0:T(4,128)(2,1)} %all-gather.3.cloned.1.call-done) | data formatting | bytes 3145728 | tf_op jit(solution)/shard_map/reshape | solution.py:49
  50.3 6.5 %fusion.4 = f32[128,1024]{1,0:T(8,128)S(1)} fusion(bf16[128,6144]{1,0:T(8,128)(2,1)S(1)} %reshape.66, bf16[1,6144,1024]{2,1,0:T(8,128)(2,1)} %param.13), kind=kOutput, calls=%fused_computation.4 | convolution fusion | flops 1610612736 | bytes 14680064 | tf_op jit(solution)/shard_map/dot_general | solution.py:50
  56.8 6.6 %fusion.13 = bf16[128,1024]{1,0:T(8,128)(2,1)S(1)} fusion(bf16[128,6144]{1,0:T(8,128)(2,1)S(1)} %reshape.66, bf16[1,6144,1024]{2,1,0:T(8,128)(2,1)} %param.14, f32[128,1024]{1,0:T(8,128)S(1)} %fusion.4), kind=kOutput, calls=%fused_computation.11 | convolution fusion | flops 1611399168 | bytes 14942208 | tf_op jit(solution)/shard_map/dot_general | solution.py:51
  63.3 0.1 dot_general.20
  63.4 7.9 %fusion.6 = bf16[8,4,4,6144]{3,2,0,1:T(4,128)(2,1)S(1)} fusion(bf16[1,1024,6144]{2,1,0:T(8,128)(2,1)} %param.15, bf16[8,4,4,1024]{3,2,1,0:T(4,128)(2,1)S(1)} %dot_general.20), kind=kOutput, calls=%fused_computation.6 | convolution fusion | flops 1611399168 | bytes 14417920 | tf_op jit(solution)/shard_map/dot_general | solution.py:53
  71.4 23.6 %all_to_all.16 = bf16[8,4,4,6144]{3,2,0,1:T(4,128)(2,1)S(1)} all-to-all(bf16[8,4,4,6144]{3,2,0,1:T(4,128)(2,1)S(1)} %fusion.6), channel_id=1, replica_groups=mesh['expert'=4,'shard'=8] {'expert'}, dimensions={1} | all-to-all | bytes 3145728 | tf_op jit(solution)/shard_map/all_to_all | solution.py:57
  95.0 0.7 copy.24
  95.7 40.4 %all_to_all.17 = bf16[8,4,4,6144]{3,2,1,0:T(4,128)(2,1)S(1)} all-to-all(bf16[8,4,4,6144]{3,2,1,0:T(4,128)(2,1)S(1)} %copy.24), channel_id=1, replica_groups=mesh['expert'=4,'shard'=8] {'shard'}, dimensions={0} | all-to-all | bytes 3145728 | tf_op jit(solution)/shard_map/all_to_all | solution.py:56
  136.1 0.9 reduce_sum.62
  137.0 1.0 fusion.9
  (3 shorter events, 0.0 us)
Async XLA Ops:
  6.5 41.0 %all-gather.3.cloned.1.call-start = ((), (), s32[]{:S(2)}) async-start(), calls=%async_computation.3 | async-start | bytes 1769472 | tf_op jit(solution)/shard_map/all_gather | solution.py:47
Sparse Core Ops, SparseCore 0:
  22.7 24.7 all-gather.2
where the time goes:
time: 145 us
  blocking collectives  74.7 us (52%)
  waiting for transfers between devices  25 us (17%)
  matrix products  23.1 us (16%)
  between operations  13.5 us (9%)
  other arithmetic  5.17 us (4%)
  local copies, waits for them, and re-layouts  3.49 us (2%)
    all_to_all x1, blocking collectives, on_device(): lax.all_to_all(lax.all_to_all(rounded_parts, 'expert', split_axis=1, conc...  40.4 us
    all_gather x1, waiting for transfers between devices, on_device(): slot_rows = lax.all_gather(arrived[None], 'shard', axis=0, tiled=True)  25 us
    all_to_all x1, blocking collectives, on_device(): lax.all_to_all(rounded_parts, 'expert', split_axis=1, concat_axis=1, tile...  23.6 us
    all_to_all x1, blocking collectives, on_device(): lax.all_to_all(buffers, 'expert', split_axis=0, concat_axis=0, tiled=True)  10.6 us
    dot_general x1, matrix products, on_device(): partial_out = jnp.dot(hidden, down_proj, preferred_element_type=jnp.float32)  7.91 us
    dot_general x1, matrix products, on_device(): up_val = jnp.dot(flat_rows, up_proj, preferred_element_type=jnp.float32)  6.57 us
    dot_general x1, matrix products, on_device(): gate_val = jnp.dot(flat_rows, gate_proj, preferred_element_type=jnp.float32)  6.49 us
  transfers between devices with their start and end apart: 1, of which 1 were waited for; matrix products, arithmetic and copies ran while one was open for 0% of the time, Pallas kernels for 0%

commit v1 on v0

--- a/solution.py
+++ b/solution.py
@@ -2,6 +2,13 @@
 import jax.numpy as jnp
 from jax import lax
 from jax.sharding import PartitionSpec as P
+
+
+def stacked_exchange(array, mesh_axis, split, join):
+    n_dev = lax.axis_size(mesh_axis)
+    blocks = jnp.stack(jnp.split(array, n_dev, axis=split), axis=0)
+    blocks = lax.all_to_all(blocks, mesh_axis, split_axis=0, concat_axis=0)
+    return jnp.concatenate(blocks, axis=join)
 
 
 def rms_norm(tokens, norm_gain):
@@ -54,7 +61,7 @@
     partial_value = partial_out.reshape(row_shape[:-1] + (down_proj.shape[1],))
     rounded_parts = partial_value.astype(jnp.bfloat16)
     pieces = lax.all_to_all(
-        lax.all_to_all(rounded_parts, "expert", split_axis=1, concat_axis=1, tiled=True),
+        stacked_exchange(rounded_parts, "expert", 1, 1),
         "shard",
         split_axis=0,
         concat_axis=0,

time: 145 us -> 145 us (level)
  no operation moved by 1% of the time
where the time goes in v1:
time: 145 us; the launch traced here: 144 us
  blocking collectives  74.7 us (52%)
  waiting for transfers between devices  25 us (17%)
  matrix products  21.7 us (15%)
  between operations  13.5 us (9%)
  other arithmetic  5.37 us (4%)
  local copies, waits for them, and re-layouts  4.11 us (3%)
    all_to_all x1, blocking collectives, on_device(): lax.all_to_all(stacked_exchange(rounded_parts, 'expert', 1, 1), 'shard',...  40.4 us
    all_gather x1, waiting for transfers between devices, on_device(): slot_rows = lax.all_gather(arrived[None], 'shard', axis=0, tiled=True)  25 us
    all_to_all x1, blocking collectives, stacked_exchange(): blocks = lax.all_to_all(blocks, mesh_axis, split_axis=0, concat_axis=0)  23.6 us
    all_to_all x1, blocking collectives, on_device(): lax.all_to_all(buffers, 'expert', split_axis=0, concat_axis=0, tiled=True)  10.6 us
    dot_general x1, matrix products, on_device(): up_val = jnp.dot(flat_rows, up_proj, preferred_element_type=jnp.float32)  6.57 us
    dot_general x1, matrix products, on_device(): gate_val = jnp.dot(flat_rows, gate_proj, preferred_element_type=jnp.float32)  6.49 us
    dot_general x1, matrix products, on_device(): partial_out = jnp.dot(hidden, down_proj, preferred_element_type=jnp.float32)  6.48 us
  transfers between devices with their start and end apart: 1, of which 1 were waited for; matrix products, arithmetic and copies ran while one was open for 0% of the time, Pallas kernels for 0%

profile of v1, /device:TPU:0, one launch (start us, length us, event | category | flops | bytes accessed | tf_op | source)
XLA Modules:
  0.0 144.3 jit_solution(18145614336359356005)
XLA Ops:
  6.5 0.0 all-gather.3.cloned.1.call-start
  6.5 1.1 fusion.17
  7.6 0.8 compare_reduce_fusion
  8.4 0.8 select_reduce_fusion.2
  9.2 0.1 select_reduce_fusion.1
  9.4 0.7 iota_compare_fusion
  10.1 0.7 convert_reduce_fusion
  10.8 1.1 convolution_convert_fusion
  11.9 10.6 %all_to_all.15 = bf16[4,4,6144]{2,1,0:T(4,128)(2,1)} all-to-all(bf16[4,4,6144]{2,1,0:T(4,128)(2,1)S(1)} %convolution_convert_fusion), channel_id=1, replica_groups=mesh['expert'=4,'shard'=8] {'expert'}, dimensions={0} | all-to-all | bytes 393216 | tf_op jit(solution)/shard_map/all_to_all | solution.py:53
  22.6 0.0 all-gather.3.cloned.1.call-update
  22.6 25.0 %all-gather.3.cloned.1.call-done = bf16[32,4,6144]{2,1,0:T(4,128)(2,1)} async-done(((bf16[4,4,6144]{2,1,0:T(4,128)(2,1)}), bf16[32,4,6144]{2,1,0:T(4,128)(2,1)}) %all-gather.3.cloned.1.call-update) | async-done | bytes 1572880 | tf_op jit(solution)/shard_map/all_gather | solution.py:54
  47.6 2.7 %reshape.72 = bf16[128,6144]{1,0:T(8,128)(2,1)S(1)} reshape(bf16[32,4,6144]{2,1,0:T(4,128)(2,1)} %all-gather.3.cloned.1.call-done) | data formatting | bytes 3145728 | tf_op jit(solution)/shard_map/reshape | solution.py:56
  50.3 6.5 %fusion.4 = f32[128,1024]{1,0:T(8,128)S(1)} fusion(bf16[128,6144]{1,0:T(8,128)(2,1)S(1)} %reshape.72, bf16[1,6144,1024]{2,1,0:T(8,128)(2,1)} %param.13), kind=kOutput, calls=%fused_computation.4 | convolution fusion | flops 1610612736 | bytes 14680064 | tf_op jit(solution)/shard_map/dot_general | solution.py:57
  56.8 6.6 %fusion.13 = bf16[128,1024]{1,0:T(8,128)(2,1)S(1)} fusion(bf16[128,6144]{1,0:T(8,128)(2,1)S(1)} %reshape.72, bf16[1,6144,1024]{2,1,0:T(8,128)(2,1)} %param.14, f32[128,1024]{1,0:T(8,128)S(1)} %fusion.4), kind=kOutput, calls=%fused_computation.12 | convolution fusion | flops 1611399168 | bytes 14942208 | tf_op jit(solution)/shard_map/dot_general | solution.py:58
  63.3 0.1 dot_general.20
  63.4 6.5 %fusion.6 = bf16[8,4,4,6144]{3,0,2,1:T(8,128)(2,1)S(1)} fusion(bf16[1,1024,6144]{2,1,0:T(8,128)(2,1)} %param.15, bf16[8,4,4,1024]{3,2,1,0:T(4,128)(2,1)S(1)} %dot_general.20), kind=kOutput, calls=%fused_computation.6 | convolution fusion | flops 1611399168 | bytes 14417920 | tf_op jit(solution)/shard_map/dot_general | solution.py:60
  69.9 0.1 slice_bitcast_fusion.3
  70.0 0.2 pad_maximum_fusion
  70.3 23.6 %all_to_all.16 = bf16[4,8,1,4,6144]{4,1,3,2,0:T(8,128)(2,1)S(1)} all-to-all(bf16[4,8,1,4,6144]{4,1,3,2,0:T(8,128)(2,1)S(1)} %pad_maximum_fusion), channel_id=1, replica_groups=mesh['expert'=4,'shard'=8] {'expert'}, dimensions={0} | all-to-all | bytes 3145728 | tf_op jit(solution)/shard_map/all_to_all | solution.py:10
  93.8 1.2 copy.21
  95.1 40.4 %all_to_all.17 = bf16[8,4,4,6144]{3,2,1,0:T(4,128)(2,1)S(1)} all-to-all(bf16[8,4,4,6144]{3,2,1,0:T(4,128)(2,1)S(1)} %copy.21), channel_id=1, replica_groups=mesh['expert'=4,'shard'=8] {'shard'}, dimensions={0} | all-to-all | bytes 3145728 | tf_op jit(solution)/shard_map/all_to_all | solution.py:63
  135.5 0.9 reduce_sum.62
  136.4 1.0 fusion.9
  (3 shorter events, 0.0 us)
Async XLA Ops:
  6.5 41.0 %all-gather.3.cloned.1.call-start = ((), (), s32[]{:S(2)}) async-start(), calls=%async_computation.3 | async-start | bytes 1769472 | tf_op jit(solution)/shard_map/all_gather | solution.py:54
Sparse Core Ops, SparseCore 0:
  22.7 24.7 all-gather.2
